TPU v7x, 32 devices: a whole 2x2x4 slice. The times are simulated.
32 devices in a mesh: seq: 4 (over z), fsdp: 8 (over y, x, core).
Axes of the slice: x: 2, y: 2, z: 4, core: 2. Of those that a mesh axis runs over, the one named last changes fastest.
Arguments:
- tokens: float32 [16, 1024, 1536], P('fsdp', 'seq'), may hold values from -6 to 6
- cotangent: float32 [16, 1024, 1536], P('fsdp', 'seq'), may hold values from -6 to 6
- attention_gain: bfloat16 [1536], P('fsdp'), may hold values from 0.5 to 1.5
- feedforward_gain: bfloat16 [1536], P('fsdp'), may hold values from 0.5 to 1.5
- query_weight: bfloat16 [1536, 1536], P('fsdp'), may hold values from -1 to 1
- key_matrix: bfloat16 [1536, 768], P('fsdp'), may hold values from -16 to 16
- value_matrix: bfloat16 [1536, 768], P('fsdp'), may hold values from -0.15625 to 0.15625
- out_weight: bfloat16 [1536, 1536], P('fsdp'), may hold values from -1.25 to 1.25
- gate_weight: bfloat16 [1536, 4096], P('fsdp'), may hold values from -0.15625 to 0.15625
- up_weight: bfloat16 [1536, 4096], P('fsdp'), may hold values from -0.15625 to 0.15625
- down_weight: bfloat16 [4096, 1536], P('fsdp'), may hold values from -0.09375 to 0.09375
Outputs:
- block_out: float32 [16, 1024, 1536], P('fsdp', 'seq')
- grad_tokens: float32 [16, 1024, 1536], P('fsdp', 'seq')
- grad_attention_gain: float32 [1536], P('fsdp')
- grad_feedforward_gain: float32 [1536], P('fsdp')
- grad_query: float32 [1536, 1536], P('fsdp')
- grad_key: float32 [1536, 768], P('fsdp')
- grad_value: float32 [1536, 768], P('fsdp')
- grad_out: float32 [1536, 1536], P('fsdp')
- grad_gate: float32 [1536, 4096], P('fsdp')
- grad_up: float32 [1536, 4096], P('fsdp')
- grad_down: float32 [4096, 1536], P('fsdp')
All inputs are finite; a program needn't handle non-finite values.
Results may differ from a plain program's by a relative error of at most 0.024.
The roundings to bfloat16 on the way count: a program that leaves them out, or rounds other values in their place, can miss the bound.
Values may be sent and summed in bfloat16 or wider, within the bound.
A program may use at most 320 MiB of HBM per device.

v0:
```python
from functools import partial
import math
import jax
import jax.numpy as jnp
from jax import lax
from jax.sharding import PartitionSpec as P

QUERY_HEADS = 16
KEY_VALUE_HEADS = 8
HEAD_DIM = 96
norm_eps = 1e-05
rope_base = 100000.0
masked_score = -1e30


def rope_tables(positions, head_size):
    half = head_size // 2
    freqs = rope_base ** (-(2.0 * jnp.arange(half, dtype=jnp.float32)) / head_size)
    angles = positions.astype(jnp.float32)[:, None] * freqs[None, :]
    return (jnp.cos(angles), jnp.sin(angles))


def rotate_halves(values, cosine, sine):
    half = values.shape[-1] // 2
    first = values[..., :half]
    second = values[..., half:]
    return jnp.concatenate(
        [first * cosine - second * sine, second * cosine + first * sine], axis=-1
    )


def reverse_rotation(grads, cosine, sine):
    half = grads.shape[-1] // 2
    first = grads[..., :half]
    second = grads[..., half:]
    return jnp.concatenate(
        [first * cosine + second * sine, second * cosine - first * sine], axis=-1
    )


def masked_scores(query_rows, key_rows, scale):
    sequence_length = query_rows.shape[0]
    scores = (
        jnp.einsum("qhgd,khd->hgqk", query_rows, key_rows, preferred_element_type=jnp.float32)
        * scale
    )
    causal = jnp.arange(sequence_length)[:, None] >= jnp.arange(sequence_length)[None, :]
    return jnp.where(causal, scores, masked_score)


def attend_items(packed_arrays, group_size, head_size):
    count, sequence_length, features = packed_arrays.shape
    kv_local = features // ((group_size + 2) * head_size)
    scale = 1.0 / math.sqrt(head_size)

    def single(item):
        split = item.reshape(sequence_length, kv_local, group_size + 2, head_size)
        query_rows = split[:, :, :group_size, :]
        key_rows = split[:, :, group_size, :]
        value_matrix_rows = split[:, :, group_size + 1, :]
        scores = masked_scores(query_rows, key_rows, scale)
        top_score = jnp.max(scores, axis=-1, keepdims=True)
        log_total = top_score + jnp.log(
            jnp.sum(jnp.exp(scores - top_score), axis=-1, keepdims=True)
        )
        probs = jnp.exp(scores - log_total).astype(jnp.bfloat16)
        attended = jnp.einsum(
            "hgqk,khd->qhgd", probs, value_matrix_rows, preferred_element_type=jnp.float32
        )
        return (
            attended.astype(jnp.bfloat16).reshape(
                sequence_length, kv_local * group_size * head_size
            ),
            log_total[..., 0],
        )

    attended_all, log_totals = lax.map(single, packed_arrays)
    return (attended_all, log_totals, packed_arrays)


def attend_back_item(inputs, group_size, head_size, cosine, sine):
    packed_item, attended_item, log_total, grad_item = inputs
    sequence_length = packed_item.shape[0]
    kv_local = packed_item.shape[1] // ((group_size + 2) * head_size)
    scale = 1.0 / math.sqrt(head_size)
    split = packed_item.reshape(sequence_length, kv_local, group_size + 2, head_size)
    query_rows = split[:, :, :group_size, :]
    key_rows = split[:, :, group_size, :]
    value_matrix_rows = split[:, :, group_size + 1, :]
    out_heads = attended_item.reshape(sequence_length, kv_local, group_size, head_size)
    grad_heads = grad_item.reshape(sequence_length, kv_local, group_size, head_size)
    scores = masked_scores(query_rows, key_rows, scale)
    probs = jnp.exp(scores - log_total[..., None])
    delta = jnp.einsum("qhgd,qhgd->hgq", grad_heads, out_heads, preferred_element_type=jnp.float32)
    value_gradients = jnp.einsum(
        "hgqk,qhgd->khd", probs.astype(jnp.bfloat16), grad_heads, preferred_element_type=jnp.float32
    )
    grad_probs = jnp.einsum(
        "qhgd,khd->hgqk", grad_heads, value_matrix_rows, preferred_element_type=jnp.float32
    )
    grad_scores = (probs * (grad_probs - delta[..., None]) * scale).astype(jnp.bfloat16)
    grad_queries = jnp.einsum(
        "hgqk,khd->qhgd", grad_scores, key_rows, preferred_element_type=jnp.float32
    )
    key_gradients = jnp.einsum(
        "hgqk,qhgd->khd", grad_scores, query_rows, preferred_element_type=jnp.float32
    )
    grad_queries = reverse_rotation(grad_queries, cosine[:, None, None, :], sine[:, None, None, :])
    key_gradients = reverse_rotation(key_gradients, cosine[:, None, :], sine[:, None, :])
    stacked = jnp.concatenate(
        [
            grad_queries.astype(jnp.bfloat16),
            key_gradients.astype(jnp.bfloat16)[:, :, None, :],
            value_gradients.astype(jnp.bfloat16)[:, :, None, :],
        ],
        axis=2,
    )
    return stacked.reshape(sequence_length, kv_local * (group_size + 2) * head_size)


def norm_back(grad_normed, normed, inverse, gain):
    scaled = grad_normed * gain
    return inverse * (scaled - normed * jnp.mean(scaled * normed, axis=-1, keepdims=True))


def body(
    tokens,
    cotangent,
    attention_gain,
    feedforward_gain,
    query_weight,
    key_matrix,
    value_matrix,
    out_weight,
    gate_weight,
    up_weight,
    down_weight,
):
    sequence_count, span_length, width = tokens.shape
    row_count = sequence_count * span_length
    group_size = QUERY_HEADS // KEY_VALUE_HEADS
    gain_low_one, gain_low_two, whole_query, whole_key, whole_value, whole_out = (
        lax.all_gather(attention_gain, "fsdp", axis=0, tiled=True),
        lax.all_gather(feedforward_gain, "fsdp", axis=0, tiled=True),
        lax.all_gather(query_weight, "fsdp", axis=0, tiled=True),
        lax.all_gather(key_matrix, "fsdp", axis=0, tiled=True),
        lax.all_gather(value_matrix, "fsdp", axis=0, tiled=True),
        lax.all_gather(out_weight, "fsdp", axis=0, tiled=True),
    )
    gain_one = gain_low_one.astype(jnp.float32)
    gain_two = gain_low_two.astype(jnp.float32)
    positions = lax.axis_index("seq") * span_length + jnp.arange(span_length, dtype=jnp.int32)
    cosine, sine = rope_tables(positions, HEAD_DIM)
    cosine_rows = jnp.tile(cosine, (sequence_count, 1))[:, None, :]
    sine_rows = jnp.tile(sine, (sequence_count, 1))[:, None, :]
    flat = tokens.reshape(row_count, width)
    inv_one = lax.rsqrt(jnp.mean(flat * flat, axis=-1, keepdims=True) + norm_eps)
    normed_one = flat * inv_one
    first_inputs = (normed_one * gain_one).astype(jnp.bfloat16)
    query_projected = jnp.dot(
        first_inputs, whole_query, preferred_element_type=jnp.float32
    ).reshape(row_count, QUERY_HEADS, HEAD_DIM)
    key_projected = jnp.dot(first_inputs, whole_key, preferred_element_type=jnp.float32).reshape(
        row_count, KEY_VALUE_HEADS, HEAD_DIM
    )
    value_matrix_rows = jnp.dot(
        first_inputs, whole_value, preferred_element_type=jnp.float32
    ).astype(jnp.bfloat16)
    query_rotated = (
        rotate_halves(query_projected, cosine_rows, sine_rows)
        .astype(jnp.bfloat16)
        .reshape(row_count, KEY_VALUE_HEADS, group_size, HEAD_DIM)
    )
    key_rotated = (
        rotate_halves(key_projected, cosine_rows, sine_rows)
        .astype(jnp.bfloat16)
        .reshape(row_count, KEY_VALUE_HEADS, 1, HEAD_DIM)
    )
    packed_arrays = jnp.concatenate(
        [
            query_rotated,
            key_rotated,
            value_matrix_rows.reshape(row_count, KEY_VALUE_HEADS, 1, HEAD_DIM),
        ],
        axis=2,
    )
    packed_arrays = packed_arrays.reshape(
        sequence_count, span_length, KEY_VALUE_HEADS * (group_size + 2) * HEAD_DIM
    )
    attend_fn = partial(attend_items, group_size=group_size, head_size=HEAD_DIM)
    heads_attended, log_totals, head_inputs = attend_fn(
        lax.all_to_all(packed_arrays, "seq", split_axis=2, concat_axis=1, tiled=True)
    )
    attended_flat = lax.all_to_all(
        heads_attended, "seq", split_axis=1, concat_axis=2, tiled=True
    ).reshape(row_count, QUERY_HEADS * HEAD_DIM)
    hidden_one = flat + jnp.dot(attended_flat, whole_out, preferred_element_type=jnp.float32)
    inv_two = lax.rsqrt(jnp.mean(hidden_one * hidden_one, axis=-1, keepdims=True) + norm_eps)
    normed_two = hidden_one * inv_two
    inputs_two = (normed_two * gain_two).astype(jnp.bfloat16)
    pieces = (
        lax.all_gather(gate_weight, "fsdp", axis=0, tiled=True),
        lax.all_gather(up_weight, "fsdp", axis=0, tiled=True),
    )
    columns = inputs_two
    gate_pre = jnp.dot(columns, pieces[0], preferred_element_type=jnp.float32)
    up_pre = jnp.dot(columns, pieces[1], preferred_element_type=jnp.float32)
    sigmoid_gate = jax.nn.sigmoid(gate_pre)
    hidden_act = (gate_pre * sigmoid_gate * up_pre).astype(jnp.bfloat16)
    columns = hidden_act
    ffn_result = jnp.dot(
        columns,
        lax.all_gather(down_weight, "fsdp", axis=0, tiled=True),
        preferred_element_type=jnp.float32,
    )
    block_out = hidden_one + ffn_result
    grad_flat = cotangent.reshape(row_count, width)
    grad_low = grad_flat.astype(jnp.bfloat16)
    grad_down = jnp.dot(hidden_act.T, grad_low, preferred_element_type=jnp.float32)
    grad_hidden = jnp.dot(
        grad_low,
        lax.all_gather(down_weight, "fsdp", axis=0, tiled=True).T,
        preferred_element_type=jnp.float32,
    )
    grad_gate_pre = (
        grad_hidden * up_pre * sigmoid_gate * (1.0 + gate_pre * (1.0 - sigmoid_gate))
    ).astype(jnp.bfloat16)
    grad_up_pre = (grad_hidden * gate_pre * sigmoid_gate).astype(jnp.bfloat16)
    grad_gate = jnp.dot(inputs_two.T, grad_gate_pre, preferred_element_type=jnp.float32)
    grad_up = jnp.dot(inputs_two.T, grad_up_pre, preferred_element_type=jnp.float32)
    pieces = (
        lax.all_gather(gate_weight, "fsdp", axis=0, tiled=True),
        lax.all_gather(up_weight, "fsdp", axis=0, tiled=True),
    )
    block = jnp.dot(grad_gate_pre, pieces[0].T, preferred_element_type=jnp.float32) + jnp.dot(
        grad_up_pre, pieces[1].T, preferred_element_type=jnp.float32
    )
    gain_grad_two = jnp.sum(block * normed_two, axis=0)
    grad_hidden_one = grad_flat + norm_back(block, normed_two, inv_two, gain_two)
    ffn_shards = (
        lax.psum_scatter(
            gain_grad_two.astype(jnp.bfloat16), "fsdp", scatter_dimension=0, tiled=True
        ).astype(jnp.float32),
        lax.psum_scatter(
            grad_gate.astype(jnp.bfloat16), "fsdp", scatter_dimension=0, tiled=True
        ).astype(jnp.float32),
        lax.psum_scatter(
            grad_up.astype(jnp.bfloat16), "fsdp", scatter_dimension=0, tiled=True
        ).astype(jnp.float32),
        lax.psum_scatter(
            grad_down.astype(jnp.bfloat16), "fsdp", scatter_dimension=0, tiled=True
        ).astype(jnp.float32),
    )
    grad_low_one = grad_hidden_one.astype(jnp.bfloat16)
    grad_out_w = jnp.dot(attended_flat.T, grad_low_one, preferred_element_type=jnp.float32)
    attended_gradient = jnp.dot(
        grad_low_one, whole_out.T, preferred_element_type=jnp.float32
    ).astype(jnp.bfloat16)
    attended_gradient = attended_gradient.reshape(
        sequence_count, span_length, QUERY_HEADS * HEAD_DIM
    )
    grad_heads = lax.all_to_all(attended_gradient, "seq", split_axis=2, concat_axis=1, tiled=True)
    full_len = grad_heads.shape[1]
    full_cos, full_sin = rope_tables(jnp.arange(full_len, dtype=jnp.int32), HEAD_DIM)
    back_fn = partial(
        attend_back_item, group_size=group_size, head_size=HEAD_DIM, cosine=full_cos, sine=full_sin
    )
    packed_grads = lax.map(back_fn, (head_inputs, heads_attended, log_totals, grad_heads))
    token_gradients = lax.all_to_all(
        packed_grads, "seq", split_axis=1, concat_axis=2, tiled=True
    ).reshape(row_count, KEY_VALUE_HEADS, group_size + 2, HEAD_DIM)
    grad_queries = token_gradients[:, :, :group_size, :].reshape(row_count, QUERY_HEADS * HEAD_DIM)
    key_gradients = token_gradients[:, :, group_size, :].reshape(
        row_count, KEY_VALUE_HEADS * HEAD_DIM
    )
    value_gradients = token_gradients[:, :, group_size + 1, :].reshape(
        row_count, KEY_VALUE_HEADS * HEAD_DIM
    )
    grad_query = jnp.dot(first_inputs.T, grad_queries, preferred_element_type=jnp.float32)
    grad_key = jnp.dot(first_inputs.T, key_gradients, preferred_element_type=jnp.float32)
    grad_value = jnp.dot(first_inputs.T, value_gradients, preferred_element_type=jnp.float32)
    grad_inputs_one = (
        jnp.dot(grad_queries, whole_query.T, preferred_element_type=jnp.float32)
        + jnp.dot(key_gradients, whole_key.T, preferred_element_type=jnp.float32)
        + jnp.dot(value_gradients, whole_value.T, preferred_element_type=jnp.float32)
    )
    gain_grad_one = jnp.sum(grad_inputs_one * normed_one, axis=0)
    grad_tokens = grad_hidden_one + norm_back(grad_inputs_one, normed_one, inv_one, gain_one)
    attn_shards = (
        lax.psum_scatter(
            gain_grad_one.astype(jnp.bfloat16), "fsdp", scatter_dimension=0, tiled=True
        ).astype(jnp.float32),
        lax.psum_scatter(
            grad_query.astype(jnp.bfloat16), "fsdp", scatter_dimension=0, tiled=True
        ).astype(jnp.float32),
        lax.psum_scatter(
            grad_key.astype(jnp.bfloat16), "fsdp", scatter_dimension=0, tiled=True
        ).astype(jnp.float32),
        lax.psum_scatter(
            grad_value.astype(jnp.bfloat16), "fsdp", scatter_dimension=0, tiled=True
        ).astype(jnp.float32),
        lax.psum_scatter(
            grad_out_w.astype(jnp.bfloat16), "fsdp", scatter_dimension=0, tiled=True
        ).astype(jnp.float32),
    )
    summed = (
        lax.psum(attn_shards[0].astype(jnp.bfloat16), "seq").astype(jnp.float32),
        lax.psum(ffn_shards[0].astype(jnp.bfloat16), "seq").astype(jnp.float32),
        lax.psum(attn_shards[1].astype(jnp.bfloat16), "seq").astype(jnp.float32),
        lax.psum(attn_shards[2].astype(jnp.bfloat16), "seq").astype(jnp.float32),
        lax.psum(attn_shards[3].astype(jnp.bfloat16), "seq").astype(jnp.float32),
        lax.psum(attn_shards[4].astype(jnp.bfloat16), "seq").astype(jnp.float32),
        lax.psum(ffn_shards[1].astype(jnp.bfloat16), "seq").astype(jnp.float32),
        lax.psum(ffn_shards[2].astype(jnp.bfloat16), "seq").astype(jnp.float32),
        lax.psum(ffn_shards[3].astype(jnp.bfloat16), "seq").astype(jnp.float32),
    )
    return (
        block_out.reshape(sequence_count, span_length, width),
        grad_tokens.reshape(sequence_count, span_length, width),
        summed[0],
        summed[1],
        summed[2],
        summed[3],
        summed[4],
        summed[5],
        summed[6],
        summed[7],
        summed[8],
    )


def solution(mesh):
    placed = (
        P("fsdp", "seq", None),
        P("fsdp", "seq", None),
        P("fsdp"),
        P("fsdp"),
        P("fsdp", None),
        P("fsdp", None),
        P("fsdp", None),
        P("fsdp", None),
        P("fsdp", None),
        P("fsdp", None),
        P("fsdp", None),
    )
    return jax.shard_map(
        body,
        mesh=mesh,
        in_specs=placed,
        out_specs=(
            P("fsdp", "seq", None),
            P("fsdp", "seq", None),
            P("fsdp"),
            P("fsdp"),
            P("fsdp", None),
            P("fsdp", None),
            P("fsdp", None),
            P("fsdp", None),
            P("fsdp", None),
            P("fsdp", None),
            P("fsdp", None),
        ),
        check_vma=False,
    )
```

profile of v0, /device:TPU:0, one launch (start us, length us, event | category | flops | bytes accessed | tf_op | source)
XLA Modules:
  0.0 1337.4 jit_solution(4431075528565036426)
XLA Ops:
  13.8 15.5 %all-reduce.5 = (bf16[1536]{0:T(1024)(128)(2,1)S(1)}, bf16[1536]{0:T(1024)(128)(2,1)S(1)}) all-reduce(bf16[1536]{0:T(1024)(128)(2,1)S(1)} %dynamic-update-slice, bf16[1536]{0:T(1024)(128)(2,1)S(1)} %dynamic-update-slice.1), channel_id=1, replica_groups=mesh['seq'=4,'fsdp'=8] {'fsdp'}, use_global_device_ids=true, to_apply=%add | all-reduce | flops 3072 | bytes 12288
  33.0 8.7 all-gather.10.cloned.1.call-done
  48.5 24.0 %all-gather.12.cloned.1.call-done = bf16[1536,768]{1,0:T(8,128)(2,1)} async-done(((bf16[192,768]{1,0:T(8,128)(2,1)}), bf16[1536,768]{1,0:T(8,128)(2,1)}) %all-gather.12.cloned.1.call-update) | async-done | bytes 2359312 | tf_op jit(solution)/shard_map/all_gather | solution.py:147
  78.4 34.8 %all-gather.8.cloned.1.call-done = bf16[1536,1536]{1,0:T(8,128)(2,1)} async-done(((bf16[192,1536]{1,0:T(8,128)(2,1)}), bf16[1536,1536]{1,0:T(8,128)(2,1)}) %all-gather.8.cloned.1.call-update) | async-done | bytes 4718608 | tf_op jit(solution)/shard_map/all_gather | solution.py:145
  134.1 71.1 %all-to-all-done = bf16[2,256,3072]{1,0,2:T(2,128)(2,1)S(1)} async-done(((bf16[2,256,3072]{1,0,2:T(2,128)(2,1)}), bf16[2,256,3072]{1,0,2:T(2,128)(2,1)S(1)}, u32[]{:S(2)}, u32[]{:S(2)}) %all-to-all-start) | async-done | bytes 3145760 | tf_op jit(solution)/shard_map/all_to_all | solution.py:192
  215.1 29.1 %while.25 = (s32[]{:T(128)}, bf16[2,1024,384]{1,2,0:T(8,128)(2,1)}, f32[2,2,2,1024]{3,2,1,0:T(2,128)S(1)}, bf16[2,1024,768]{1,2,0:T(8,128)(2,1)S(1)}, s32[]{:T(128)}) while((s32[]{:T(128)}, bf16[2,1024,384]{1,2,0:T(8,128)(2,1)}, f32[2,2,2,1024]{3,2,1,0:T(2,128)S(1)}, bf16[2,1024,768]{1,2,0:T(8,128)(2,1)S(1)}, s32[]{:T(128)}) %tuple.80), condition=%wide.region_4.5_spmd, body=%wide.region_1.4_spmd.sunk | while | flops 1658187776 | bytes 68026976 | solution.py:77
  256.9 33.5 %all-to-all-done.1 = bf16[2,1024,384]{2,0,1:T(2,128)(2,1)} async-done(((bf16[2,1024,384]{2,0,1:T(2,128)(2,1)}), bf16[2,1024,384]{2,0,1:T(2,128)(2,1)}, u32[]{:S(2)}, u32[]{:S(2)}) %all-to-all-start.1) | async-done | bytes 1572896 | tf_op jit(solution)/shard_map/all_to_all | solution.py:194
  304.1 12.1 fusion.46
  316.2 12.2 fusion.47
  328.4 46.9 %all-gather.20.cloned.1.call-done = bf16[4096,1536]{1,0:T(8,128)(2,1)} async-done(((bf16[512,1536]{1,0:T(8,128)(2,1)}), bf16[4096,1536]{1,0:T(8,128)(2,1)}) %all-gather.20.cloned.1.call-update) | async-done | bytes 12582928 | tf_op jit(solution)/shard_map/all_gather | solution.py:213
  375.2 19.2 %multiply_convert_fusion = (bf16[512,4096]{1,0:T(8,128)(2,1)}, bf16[512,4096]{1,0:T(8,128)(2,1)}, bf16[512,4096]{1,0:T(8,128)(2,1)}) fusion(f32[512,4096]{1,0:T(8,128)} %fusion.46, f32[512,4096]{1,0:T(8,128)} %fusion.47, bf16[512,1536]{1,0:T(8,128)(2,1)} %bitcast_convert_fusion, bf16[4096,1536]{1,0:T(8,128)(2,1)} %all-gather.20.cloned.1.call-done), kind=kOutput, calls=%fused_computation.61 | convolution fusion | flops 6476005376 | bytes 43515904 | tf_op jit(solution)/shard_map/dot_general | solution.py:220
  394.4 11.2 fusion.48
  405.7 12.0 multiply_reduce_fusion
  442.4 30.3 %all-to-all-done.2 = bf16[2,256,1536]{1,0,2:T(2,128)(2,1)} async-done(((bf16[2,256,1536]{1,0,2:T(2,128)(2,1)}), bf16[2,256,1536]{1,0,2:T(2,128)(2,1)}, u32[]{:S(2)}, u32[]{:S(2)}) %all-to-all-start.2) | async-done | bytes 1572896 | tf_op jit(solution)/shard_map/all_to_all | solution.py:262
  480.3 73.4 %while.26 = (s32[]{:T(128)}, bf16[2,1024,768]{1,2,0:T(8,128)(2,1)}, bf16[2,1024,768]{1,2,0:T(8,128)(2,1)S(1)}, f32[2,2,2,1024]{3,2,1,0:T(2,128)S(1)}, bf16[2,102...) while((s32[]{:T(128)}, bf16[2,1024,768]{1,2,0:T(8,128)(2,1)}, ...), condition=%wide.region_8.9_spmd.clone.clone.clone, body=%wide.region_7.8_spmd.clone.clone.clone.sunk | while | flops 4085755904 | bytes 115446648 | solution.py:268
  482.4 8.3 fusion.118
  491.0 10.1 fusion.121
  527.4 10.0 fusion.121
  561.3 73.6 %all_to_all.66 = bf16[2,1024,768]{2,0,1:T(2,128)(2,1)} all-to-all(bf16[2,1024,768]{2,0,1:T(2,128)(2,1)S(1)} %copy.81), channel_id=1, replica_groups=mesh['seq'=4,'fsdp'=8] {'seq'}, dimensions={1} | all-to-all | bytes 6291456 | tf_op jit(solution)/shard_map/all_to_all | solution.py:269
  634.9 11.2 copy.82
  667.9 11.8 convolution_convert_fusion.2
  679.8 11.9 convolution_convert_fusion.1
  693.1 11.9 convolution_convert_fusion
  705.1 37.1 %reduce-scatter.12.cloned.1.call-done = bf16[192,768]{1,0:T(8,128)(2,1)} async-done(((bf16[1536,768]{1,0:T(8,128)(2,1)}), bf16[192,768]{1,0:T(8,128)(2,1)}) %reduce-scatter.12.cloned.1.call-update) | async-done | bytes 294928 | tf_op jit(solution)/shard_map/reduce_scatter | solution.py:299
  742.2 57.3 %reduce-scatter.8.cloned.1.call-done = bf16[192,1536]{1,0:T(8,128)(2,1)} async-done(((bf16[1536,1536]{1,0:T(8,128)(2,1)}), bf16[192,1536]{1,0:T(8,128)(2,1)}) %reduce-scatter.8.cloned.1.call-update) | async-done | bytes 589840 | tf_op jit(solution)/shard_map/reduce_scatter | solution.py:293
  799.5 95.7 %reduce-scatter.16.cloned.1.call-done = bf16[192,4096]{1,0:T(8,128)(2,1)} async-done(((bf16[1536,4096]{1,0:T(8,128)(2,1)}), bf16[192,4096]{1,0:T(8,128)(2,1)}) %reduce-scatter.16.cloned.1.call-update) | async-done | bytes 1572880 | tf_op jit(solution)/shard_map/reduce_scatter | solution.py:244
  895.2 95.8 %reduce-scatter.18.cloned.1.call-done = bf16[192,4096]{1,0:T(8,128)(2,1)} async-done(((bf16[1536,4096]{1,0:T(8,128)(2,1)}), bf16[192,4096]{1,0:T(8,128)(2,1)}) %reduce-scatter.18.cloned.1.call-update) | async-done | bytes 1572880 | tf_op jit(solution)/shard_map/reduce_scatter | solution.py:247
  991.0 95.7 %reduce-scatter.20.cloned.1.call-done = bf16[512,1536]{1,0:T(8,128)(2,1)} async-done(((bf16[4096,1536]{1,0:T(8,128)(2,1)}), bf16[512,1536]{1,0:T(8,128)(2,1)}) %reduce-scatter.20.cloned.1.call-update) | async-done | bytes 1572880 | tf_op jit(solution)/shard_map/reduce_scatter | solution.py:250
  1088.5 12.2 convolution_add_fusion.3
  1112.1 13.6 %all-reduce.4 = (bf16[1536]{0:T(1024)(128)(2,1)S(1)}, bf16[1536]{0:T(1024)(128)(2,1)S(1)}) all-reduce(bf16[1536]{0:T(1024)(128)(2,1)S(1)} %get-tuple-element.208, bf16[1536]{0:T(1024)(128)(2,1)S(1)} %copy-done.38), channel_id=2, replica_groups=mesh['seq'=4,'fsdp'=8] {'fsdp'}, use_global_device_ids=true, to_apply=%region_11.12.clone | all-reduce | flops 3072 | bytes 12288
  1125.8 12.3 all-reduce.6
  1144.5 174.5 %all-reduce.10.cloned.1.call-done = (bf16[192,1536]{1,0:T(8,128)(2,1)}, bf16[192,768]{1,0:T(8,128)(2,1)}, bf16[192,768]{1,0:T(8,128)(2,1)}, bf16[192,1536]{1,0:T...) async-done(((bf16[192,1536]{1,0:T(8,128)(2,1)}, bf16[192,768]{1,0:T(8,128)(2,1)}, bf16[192,768]{1,0:T(8,128)(2,1)}, ...) | async-done | bytes 6488080 | tf_op jit(solution)/shard_map/psum | solution.py:309
  (245 shorter events, 246.1 us)
Async XLA Ops:
  7.2 34.6 %all-gather.10.cloned.1.call-start = ((), (), s32[]{:S(2)}) async-start(), calls=%async_computation.12 | async-start | bytes 2654208 | tf_op jit(solution)/shard_map/all_gather | solution.py:146
  7.9 5.6 copy-start.41
  7.9 21.4 %copy-start = (f32[2,256,1536]{2,1,0:T(8,128)S(1)}, f32[2,256,1536]{2,1,0:T(8,128)}, u32[]{:S(2)}) copy-start(f32[2,256,1536]{2,1,0:T(8,128)} %param.15) | copy-start | bytes 9437188
  8.0 64.6 %all-gather.12.cloned.1.call-start = ((), (), s32[]{:S(2)}) async-start(), calls=%async_computation.13 | async-start | bytes 2654208 | tf_op jit(solution)/shard_map/all_gather | solution.py:147
  8.7 104.5 %all-gather.8.cloned.1.call-start = ((), (), s32[]{:S(2)}) async-start(), calls=%async_computation.11 | async-start | bytes 5308416 | tf_op jit(solution)/shard_map/all_gather | solution.py:145
  9.4 285.0 %all-gather.14.cloned.1.call-start = ((), (), s32[]{:S(2)}) async-start(), calls=%async_computation.14 | async-start | bytes 5308416 | tf_op jit(solution)/shard_map/all_gather | solution.py:148
  10.0 294.1 %all-gather.16.cloned.1.call-start = ((), (), s32[]{:S(2)}) async-start(), calls=%async_computation.15 | async-start | bytes 14155776 | tf_op jit(solution)/shard_map/all_gather | solution.py:202
  10.6 305.6 %all-gather.18.cloned.1.call-start = ((), (), s32[]{:S(2)}) async-start(), calls=%async_computation.16 | async-start | bytes 14155776 | tf_op jit(solution)/shard_map/all_gather | solution.py:203
  11.2 364.1 %all-gather.20.cloned.1.call-start = ((), (), s32[]{:S(2)}) async-start(), calls=%async_computation.17 | async-start | bytes 14155776 | tf_op jit(solution)/shard_map/all_gather | solution.py:213
  12.0 18.0 %copy-start.36 = (f32[48]{0:T(128)}, f32[48]{0:T(128)S(1)}, u32[]{:S(2)}) copy-start(f32[48]{0:T(128)S(1)} %multiply_power_fusion) | copy-start | bytes 580
  48.5 28.7 %copy-start.20 = (f32[512,8,96]{0,2,1:T(8,128)S(1)}, f32[512,8,96]{0,2,1:T(8,128)}, u32[]{:S(2)}) copy-start(f32[512,8,96]{0,2,1:T(8,128)} %fusion.45) | copy-start | bytes 4718596
  113.2 6.8 copy-start.21
  129.3 75.8 %all-to-all-start = ((bf16[2,256,3072]{1,0,2:T(2,128)(2,1)}), bf16[2,256,3072]{1,0,2:T(2,128)(2,1)S(1)}, u32[]{:S(2)}, u32[]{:S(2)}) async-start(bf16[2,256,3072]{1,0,2:T(2,128)(2,1)} %reshape.346), calls=%async_computation | async-start | bytes 6291456 | tf_op jit(solution)/shard_map/all_to_all | solution.py:192
  249.1 41.3 %all-to-all-start.1 = ((bf16[2,1024,384]{2,0,1:T(2,128)(2,1)}), bf16[2,1024,384]{2,0,1:T(2,128)(2,1)}, u32[]{:S(2)}, u32[]{:S(2)}) async-start(bf16[2,1024,384]{2,0,1:T(2,128)(2,1)} %copy.76), calls=%async_computation.1 | async-start | bytes 3145728 | tf_op jit(solution)/shard_map/all_to_all | solution.py:194
  394.4 11.2 copy-start.9
  405.6 12.0 copy-start.6
  418.4 7.3 copy-start.7
  430.6 42.1 %all-to-all-start.2 = ((bf16[2,256,1536]{1,0,2:T(2,128)(2,1)}), bf16[2,256,1536]{1,0,2:T(2,128)(2,1)}, u32[]{:S(2)}, u32[]{:S(2)}) async-start(bf16[2,256,1536]{1,0,2:T(2,128)(2,1)} %copy.78), calls=%async_computation.2 | async-start | bytes 3145728 | tf_op jit(solution)/shard_map/all_to_all | solution.py:262
  435.2 270.0 %reduce-scatter.14.cloned.1.call-start = ((), (), s32[]{:S(2)}) async-start(), calls=%async_computation.21 | async-start | bytes 5308416 | tf_op jit(solution)/shard_map/reduce_scatter | solution.py:302
  442.3 262.8 %reduce-scatter.10.cloned.1.call-start = ((), (), s32[]{:S(2)}) async-start(), calls=%async_computation.19 | async-start | bytes 2654208 | tf_op jit(solution)/shard_map/reduce_scatter | solution.py:296
  472.6 7.6 copy-start.37
  491.0 10.2 copy-start.4
  507.3 8.3 copy-start.3
  527.4 10.0 copy-start.4
  543.6 8.3 copy-start.3
  655.4 86.8 %reduce-scatter.12.cloned.1.call-start = ((), (), s32[]{:S(2)}) async-start(), calls=%async_computation.20 | async-start | bytes 2654208 | tf_op jit(solution)/shard_map/reduce_scatter | solution.py:299
  659.9 139.6 %reduce-scatter.8.cloned.1.call-start = ((), (), s32[]{:S(2)}) async-start(), calls=%async_computation.18 | async-start | bytes 5308416 | tf_op jit(solution)/shard_map/reduce_scatter | solution.py:293
  666.5 228.7 %reduce-scatter.16.cloned.1.call-start = ((), (), s32[]{:S(2)}) async-start(), calls=%async_computation.22 | async-start | bytes 14155776 | tf_op jit(solution)/shard_map/reduce_scatter | solution.py:244
  679.8 311.2 %reduce-scatter.18.cloned.1.call-start = ((), (), s32[]{:S(2)}) async-start(), calls=%async_computation.23 | async-start | bytes 14155776 | tf_op jit(solution)/shard_map/reduce_scatter | solution.py:247
  691.7 394.9 %reduce-scatter.20.cloned.1.call-start = ((), (), s32[]{:S(2)}) async-start(), calls=%async_computation.24 | async-start | bytes 14155776 | tf_op jit(solution)/shard_map/reduce_scatter | solution.py:250
  705.0 614.0 %all-reduce.10.cloned.1.call-start = ((), (), s32[]{:S(2)}) async-start(), calls=%async_computation.25 | async-start | bytes 12976128 | tf_op jit(solution)/shard_map/psum | solution.py:309
  1088.5 12.2 copy-start.19
  (32 other events, 85.5 us)
Sparse Core Ops, SparseCore 0:
  9.9 31.8 all-gather.9
  43.6 28.8 all-gather.11
  74.4 38.7 all-gather.7
  115.0 38.7 all-gather.13
  155.5 71.9 all-gather.15
  229.3 71.9 all-gather.17
  303.2 71.9 all-gather.19
  442.5 54.2 reduce-scatter.13
  655.5 40.4 reduce-scatter.9
  699.8 42.3 reduce-scatter.11
  745.7 53.7 reduce-scatter.7
  802.8 92.2 reduce-scatter.15
  898.7 92.2 reduce-scatter.17
  994.3 92.2 reduce-scatter.19
  1089.4 229.5 all-reduce.9
where the time goes:
time: 1340 us
  waiting for transfers between devices  810 us (60%)
  matrix products  249 us (19%)
  blocking collectives  115 us (9%)
  local copies, waits for them, and re-layouts  89.6 us (7%)
  other arithmetic  42.4 us (3%)
  between operations  16.2 us (1%)
  starting transfers between devices  14.4 us (1%)
    psum x1, waiting for transfers between devices, body(): lax.psum(attn_shards[1].astype(jnp.bfloat16), 'seq').astype(jnp.float32)  175 us
    reduce_scatter x1, waiting for transfers between devices, body(): lax.psum_scatter(grad_up.astype(jnp.bfloat16), 'fsdp', scatter_dimension=...  95.8 us
    reduce_scatter x1, waiting for transfers between devices, body(): lax.psum_scatter(grad_gate.astype(jnp.bfloat16), 'fsdp', scatter_dimensio...  95.7 us
    reduce_scatter x1, waiting for transfers between devices, body(): lax.psum_scatter(grad_down.astype(jnp.bfloat16), 'fsdp', scatter_dimensio...  95.7 us
    all_to_all x1, blocking collectives, body(): lax.all_to_all(packed_grads, 'seq', split_axis=1, concat_axis=2, tiled=True)  73.6 us
    all_to_all x1, waiting for transfers between devices, body(): lax.all_to_all(packed_arrays, 'seq', split_axis=2, concat_axis=1, tiled=T...  71.1 us
    reduce_scatter x1, waiting for transfers between devices, body(): lax.psum_scatter(grad_query.astype(jnp.bfloat16), 'fsdp', scatter_dimensi...  57.3 us
    all_gather x1, waiting for transfers between devices, body(): lax.all_gather(down_weight, 'fsdp', axis=0, tiled=True)  46.9 us
  transfers between devices with their start and end apart: 18, of which 13 were waited for; matrix products, arithmetic and copies ran while one was open for 22% of the time, Pallas kernels for 0%

commit v1 on v0

--- a/solution.py
+++ b/solution.py
@@ -11,6 +11,29 @@
 norm_eps = 1e-05
 rope_base = 100000.0
 masked_score = -1e30
+
+
+def in_blocks(value, dim, size):
+    shape = value.shape
+    blocks = value.reshape(*shape[:dim], size, shape[dim] // size, *shape[dim + 1 :])
+    return jnp.moveaxis(blocks, dim, 0)
+
+
+def in_order(parts, dim):
+    lengths = list(parts.shape[1:])
+    lengths[dim] *= parts.shape[0]
+    return jnp.moveaxis(parts, 0, dim).reshape(lengths)
+
+
+def pairwise_exchange(array, axis, split_dim, concat_dim):
+    size, here = (lax.axis_size(axis), lax.axis_index(axis))
+    blocks = in_blocks(array, split_dim, size)
+    outs = [blocks[here]]
+    for step in range(1, size):
+        sent = blocks[here ^ step]
+        outs.append(lax.ppermute(sent, axis, [(i, i ^ step) for i in range(size)]))
+    blocks = jnp.stack(outs)[here ^ jnp.arange(size)]
+    return in_order(blocks, concat_dim)
 
 
 def rope_tables(positions, head_size):
@@ -189,7 +212,7 @@
     )
     attend_fn = partial(attend_items, group_size=group_size, head_size=HEAD_DIM)
     heads_attended, log_totals, head_inputs = attend_fn(
-        lax.all_to_all(packed_arrays, "seq", split_axis=2, concat_axis=1, tiled=True)
+        pairwise_exchange(packed_arrays, "seq", 2, 1)
     )
     attended_flat = lax.all_to_all(
         heads_attended, "seq", split_axis=1, concat_axis=2, tiled=True

time: 1340 us -> 1350 us (level)
  waiting for transfers between devices: 810 us -> 778 us
  local copies, waits for them, and re-layouts: 89.6 us -> 104 us
  starting transfers between devices: 14.4 us -> 28.7 us
    all_to_all x1 -> x0, waiting for transfers between devices: 71.1 us -> none  [body(): lax.all_to_all(packed_arrays, 'seq', split_axis=2, concat_axis=1, tiled=T...]
    ppermute x0 -> x3, waiting for transfers between devices: none -> 48.6 us  [pairwise_exchange(): outs.append(lax.ppermute(sent, axis, [(i, i ^ step) for i in range(size)]))]
    all_to_all x1, starting transfers between devices: 4.58 us -> 19.1 us  [body(): lax.all_to_all(heads_attended, 'seq', split_axis=1, concat_axis=2, tiled=...]
  transfers between devices with their start and end apart: 18 -> 20, of which waited for: 13 -> 14; matrix products, arithmetic and copies ran while one was open for 22% -> 24% of each run, Pallas kernels for 0% -> 0%
where the time goes in v1:
time: 1350 us; the launch traced here: 1340 us
  waiting for transfers between devices  778 us (58%)
  matrix products  249 us (18%)
  blocking collectives  115 us (9%)
  local copies, waits for them, and re-layouts  104 us (8%)
  other arithmetic  46 us (3%)
  starting transfers between devices  28.7 us (2%)
  between operations  16.3 us (1%)
    psum x1, waiting for transfers between devices, body(): lax.psum(attn_shards[1].astype(jnp.bfloat16), 'seq').astype(jnp.float32)  174 us
    reduce_scatter x1, waiting for transfers between devices, body(): lax.psum_scatter(grad_up.astype(jnp.bfloat16), 'fsdp', scatter_dimension=...  95.8 us
    reduce_scatter x1, waiting for transfers between devices, body(): lax.psum_scatter(grad_down.astype(jnp.bfloat16), 'fsdp', scatter_dimensio...  95.7 us
    reduce_scatter x1, waiting for transfers between devices, body(): lax.psum_scatter(grad_gate.astype(jnp.bfloat16), 'fsdp', scatter_dimensio...  95.7 us
    all_to_all x1, blocking collectives, body(): lax.all_to_all(packed_grads, 'seq', split_axis=1, concat_axis=2, tiled=True)  73.5 us
    reduce_scatter x1, waiting for transfers between devices, body(): lax.psum_scatter(grad_query.astype(jnp.bfloat16), 'fsdp', scatter_dimensi...  57.3 us
    ppermute x3, waiting for transfers between devices, pairwise_exchange(): outs.append(lax.ppermute(sent, axis, [(i, i ^ step) for i in range(size)]))  48.6 us
    all_gather x1, waiting for transfers between devices, body(): lax.all_gather(down_weight, 'fsdp', axis=0, tiled=True)  37.4 us
  transfers between devices with their start and end apart: 20, of which 14 were waited for; matrix products, arithmetic and copies ran while one was open for 24% of the time, Pallas kernels for 0%

profile of v1, /device:TPU:0, one launch (start us, length us, event | category | flops | bytes accessed | tf_op | source)
XLA Modules:
  0.0 1337.3 jit_solution(18415690330121915946)
XLA Ops:
  13.8 15.5 %all-reduce.5 = (bf16[1536]{0:T(1024)(128)(2,1)S(1)}, bf16[1536]{0:T(1024)(128)(2,1)S(1)}) all-reduce(bf16[1536]{0:T(1024)(128)(2,1)S(1)} %dynamic-update-slice, bf16[1536]{0:T(1024)(128)(2,1)S(1)} %dynamic-update-slice.1), channel_id=1, replica_groups=mesh['seq'=4,'fsdp'=8] {'fsdp'}, use_global_device_ids=true, to_apply=%add | all-reduce | flops 3072 | bytes 12288
  44.6 28.0 %all-gather.12.cloned.1.call-done = bf16[1536,768]{1,0:T(8,128)(2,1)} async-done(((bf16[192,768]{1,0:T(8,128)(2,1)}), bf16[1536,768]{1,0:T(8,128)(2,1)}) %all-gather.12.cloned.1.call-update) | async-done | bytes 2359312 | tf_op jit(solution)/shard_map/all_gather | solution.py:170
  81.5 31.7 %all-gather.8.cloned.1.call-done = bf16[1536,1536]{1,0:T(8,128)(2,1)} async-done(((bf16[192,1536]{1,0:T(8,128)(2,1)}), bf16[1536,1536]{1,0:T(8,128)(2,1)}) %all-gather.8.cloned.1.call-update) | async-done | bytes 4718608 | tf_op jit(solution)/shard_map/all_gather | solution.py:168
  148.2 22.5 %collective-permute-done = bf16[2,256,768]{2,1,0:T(8,128)(2,1)S(1)} collective-permute-done((bf16[2,256,768]{2,1,0:T(8,128)(2,1)}, bf16[2,256,768]{2,1,0:T(8,128)(2,1)S(1)}, u32[]{:S(2)}, u32[]{:S(2)}) %collective-permute-start) | collective-permute-done | bytes 786464 | tf_op jit(solution)/shard_map/ppermute | solution.py:34
  170.7 26.1 %collective-permute-done.1 = bf16[2,256,768]{2,1,0:T(8,128)(2,1)S(1)} collective-permute-done((bf16[2,256,768]{2,1,0:T(8,128)(2,1)}, bf16[2,256,768]{2,1,0:T(8,128)(2,1)S(1)}, u32[]{:S(2)}, u32[]{:S(2)}) %collective-permute-start.1) | collective-permute-done | bytes 786464 | tf_op jit(solution)/shard_map/ppermute | solution.py:34
  209.4 29.2 %while.25 = (s32[]{:T(128)}, bf16[2,1024,384]{1,2,0:T(8,128)(2,1)}, f32[2,2,2,1024]{3,2,1,0:T(2,128)S(1)}, bf16[2,1024,768]{1,2,0:T(8,128)(2,1)S(1)}, s32[]{:T(128)}) while((s32[]{:T(128)}, bf16[2,1024,384]{1,2,0:T(8,128)(2,1)}, f32[2,2,2,1024]{3,2,1,0:T(2,128)S(1)}, bf16[2,1024,768]{1,2,0:T(8,128)(2,1)S(1)}, s32[]{:T(128)}) %tuple.83), condition=%wide.region_4.5_spmd, body=%wide.region_1.4_spmd.sunk | while | flops 1658187776 | bytes 68026976 | solution.py:100
  243.6 19.1 %all-to-all-start = ((bf16[2,1024,384]{2,0,1:T(2,128)(2,1)}), bf16[2,1024,384]{2,0,1:T(2,128)(2,1)}, u32[]{:S(2)}, u32[]{:S(2)}) async-start(bf16[2,1024,384]{2,0,1:T(2,128)(2,1)} %copy.86), calls=%async_computation | async-start | bytes 3145728 | tf_op jit(solution)/shard_map/all_to_all | solution.py:217
  266.9 33.0 %all-to-all-done = bf16[2,1024,384]{2,0,1:T(2,128)(2,1)} async-done(((bf16[2,1024,384]{2,0,1:T(2,128)(2,1)}), bf16[2,1024,384]{2,0,1:T(2,128)(2,1)}, u32[]{:S(2)}, u32[]{:S(2)}) %all-to-all-start) | async-done | bytes 1572896 | tf_op jit(solution)/shard_map/all_to_all | solution.py:217
  313.6 12.1 fusion.47
  325.7 12.2 fusion.48
  337.9 37.4 %all-gather.20.cloned.1.call-done = bf16[4096,1536]{1,0:T(8,128)(2,1)} async-done(((bf16[512,1536]{1,0:T(8,128)(2,1)}), bf16[4096,1536]{1,0:T(8,128)(2,1)}) %all-gather.20.cloned.1.call-update) | async-done | bytes 12582928 | tf_op jit(solution)/shard_map/all_gather | solution.py:236
  375.2 19.2 %multiply_convert_fusion = (bf16[512,4096]{1,0:T(8,128)(2,1)}, bf16[512,4096]{1,0:T(8,128)(2,1)}, bf16[512,4096]{1,0:T(8,128)(2,1)}) fusion(f32[512,4096]{1,0:T(8,128)} %fusion.47, f32[512,4096]{1,0:T(8,128)} %fusion.48, bf16[512,1536]{1,0:T(8,128)(2,1)} %bitcast_convert_fusion, bf16[4096,1536]{1,0:T(8,128)(2,1)} %all-gather.20.cloned.1.call-done), kind=kOutput, calls=%fused_computation.62 | convolution fusion | flops 6476005376 | bytes 43515904 | tf_op jit(solution)/shard_map/dot_general | solution.py:243
  394.4 10.9 fusion.49
  405.4 12.0 multiply_reduce_fusion
  442.1 30.2 %all-to-all-done.1 = bf16[2,256,1536]{1,0,2:T(2,128)(2,1)} async-done(((bf16[2,256,1536]{1,0,2:T(2,128)(2,1)}), bf16[2,256,1536]{1,0,2:T(2,128)(2,1)}, u32[]{:S(2)}, u32[]{:S(2)}) %all-to-all-start.1) | async-done | bytes 1572896 | tf_op jit(solution)/shard_map/all_to_all | solution.py:285
  480.0 73.4 %while.26 = (s32[]{:T(128)}, bf16[2,1024,768]{1,2,0:T(8,128)(2,1)}, bf16[2,1024,768]{1,2,0:T(8,128)(2,1)S(1)}, f32[2,2,2,1024]{3,2,1,0:T(2,128)S(1)}, bf16[2,102...) while((s32[]{:T(128)}, bf16[2,1024,768]{1,2,0:T(8,128)(2,1)}, ...), condition=%wide.region_8.9_spmd.clone.clone.clone, body=%wide.region_7.8_spmd.clone.clone.clone.sunk | while | flops 4085755904 | bytes 115446648 | solution.py:291
  491.0 10.1 fusion.122
  527.3 10.0 fusion.122
  561.0 73.5 %all_to_all.48 = bf16[2,1024,768]{2,0,1:T(2,128)(2,1)} all-to-all(bf16[2,1024,768]{2,0,1:T(2,128)(2,1)S(1)} %copy.91), channel_id=1, replica_groups=mesh['seq'=4,'fsdp'=8] {'seq'}, dimensions={1} | all-to-all | bytes 6291456 | tf_op jit(solution)/shard_map/all_to_all | solution.py:292
  634.6 11.2 copy.92
  667.6 11.8 convolution_convert_fusion.2
  679.5 11.9 convolution_convert_fusion.1
  692.8 12.1 convolution_convert_fusion
  705.0 36.9 %reduce-scatter.12.cloned.1.call-done = bf16[192,768]{1,0:T(8,128)(2,1)} async-done(((bf16[1536,768]{1,0:T(8,128)(2,1)}), bf16[192,768]{1,0:T(8,128)(2,1)}) %reduce-scatter.12.cloned.1.call-update) | async-done | bytes 294928 | tf_op jit(solution)/shard_map/reduce_scatter | solution.py:322
  741.9 57.3 %reduce-scatter.8.cloned.1.call-done = bf16[192,1536]{1,0:T(8,128)(2,1)} async-done(((bf16[1536,1536]{1,0:T(8,128)(2,1)}), bf16[192,1536]{1,0:T(8,128)(2,1)}) %reduce-scatter.8.cloned.1.call-update) | async-done | bytes 589840 | tf_op jit(solution)/shard_map/reduce_scatter | solution.py:316
  799.2 95.7 %reduce-scatter.16.cloned.1.call-done = bf16[192,4096]{1,0:T(8,128)(2,1)} async-done(((bf16[1536,4096]{1,0:T(8,128)(2,1)}), bf16[192,4096]{1,0:T(8,128)(2,1)}) %reduce-scatter.16.cloned.1.call-update) | async-done | bytes 1572880 | tf_op jit(solution)/shard_map/reduce_scatter | solution.py:267
  894.8 95.8 %reduce-scatter.18.cloned.1.call-done = bf16[192,4096]{1,0:T(8,128)(2,1)} async-done(((bf16[1536,4096]{1,0:T(8,128)(2,1)}), bf16[192,4096]{1,0:T(8,128)(2,1)}) %reduce-scatter.18.cloned.1.call-update) | async-done | bytes 1572880 | tf_op jit(solution)/shard_map/reduce_scatter | solution.py:270
  990.6 95.7 %reduce-scatter.20.cloned.1.call-done = bf16[512,1536]{1,0:T(8,128)(2,1)} async-done(((bf16[4096,1536]{1,0:T(8,128)(2,1)}), bf16[512,1536]{1,0:T(8,128)(2,1)}) %reduce-scatter.20.cloned.1.call-update) | async-done | bytes 1572880 | tf_op jit(solution)/shard_map/reduce_scatter | solution.py:273
  1088.2 12.3 convolution_add_fusion.3
  1111.8 13.6 %all-reduce.4 = (bf16[1536]{0:T(1024)(128)(2,1)S(1)}, bf16[1536]{0:T(1024)(128)(2,1)S(1)}) all-reduce(bf16[1536]{0:T(1024)(128)(2,1)S(1)} %get-tuple-element.208, bf16[1536]{0:T(1024)(128)(2,1)S(1)} %copy-done.40), channel_id=2, replica_groups=mesh['seq'=4,'fsdp'=8] {'fsdp'}, use_global_device_ids=true, to_apply=%region_11.12.clone | all-reduce | flops 3072 | bytes 12288
  1125.5 12.3 all-reduce.6
  1144.3 174.4 %all-reduce.10.cloned.1.call-done = (bf16[192,1536]{1,0:T(8,128)(2,1)}, bf16[192,768]{1,0:T(8,128)(2,1)}, bf16[192,768]{1,0:T(8,128)(2,1)}, bf16[192,1536]{1,0:T...) async-done(((bf16[192,1536]{1,0:T(8,128)(2,1)}, bf16[192,768]{1,0:T(8,128)(2,1)}, bf16[192,768]{1,0:T(8,128)(2,1)}, ...) | async-done | bytes 6488080 | tf_op jit(solution)/shard_map/psum | solution.py:332
  (261 shorter events, 275.4 us)
Async XLA Ops:
  7.2 34.6 %all-gather.10.cloned.1.call-start = ((), (), s32[]{:S(2)}) async-start(), calls=%async_computation.11 | async-start | bytes 2654208 | tf_op jit(solution)/shard_map/all_gather | solution.py:169
  7.9 64.6 %all-gather.12.cloned.1.call-start = ((), (), s32[]{:S(2)}) async-start(), calls=%async_computation.12 | async-start | bytes 2654208 | tf_op jit(solution)/shard_map/all_gather | solution.py:170
  8.7 104.5 %all-gather.8.cloned.1.call-start = ((), (), s32[]{:S(2)}) async-start(), calls=%async_computation.10 | async-start | bytes 5308416 | tf_op jit(solution)/shard_map/all_gather | solution.py:168
  9.4 20.5 %copy-start = (f32[2,256,1536]{2,1,0:T(8,128)S(1)}, f32[2,256,1536]{2,1,0:T(8,128)}, u32[]{:S(2)}) copy-start(f32[2,256,1536]{2,1,0:T(8,128)} %param.15) | copy-start | bytes 9437188
  9.4 294.5 %all-gather.14.cloned.1.call-start = ((), (), s32[]{:S(2)}) async-start(), calls=%async_computation.13 | async-start | bytes 5308416 | tf_op jit(solution)/shard_map/all_gather | solution.py:171
  10.0 303.5 %all-gather.16.cloned.1.call-start = ((), (), s32[]{:S(2)}) async-start(), calls=%async_computation.14 | async-start | bytes 14155776 | tf_op jit(solution)/shard_map/all_gather | solution.py:225
  10.6 315.1 %all-gather.18.cloned.1.call-start = ((), (), s32[]{:S(2)}) async-start(), calls=%async_computation.15 | async-start | bytes 14155776 | tf_op jit(solution)/shard_map/all_gather | solution.py:226
  11.2 364.1 %all-gather.20.cloned.1.call-start = ((), (), s32[]{:S(2)}) async-start(), calls=%async_computation.16 | async-start | bytes 14155776 | tf_op jit(solution)/shard_map/all_gather | solution.py:236
  134.0 10.0 copy-start.16
  134.0 12.4 copy-start.15
  137.2 33.5 %collective-permute-start = (bf16[2,256,768]{2,1,0:T(8,128)(2,1)}, bf16[2,256,768]{2,1,0:T(8,128)(2,1)S(1)}, u32[]{:S(2)}, u32[]{:S(2)}) collective-permute-start(bf16[2,256,768]{2,1,0:T(8,128)(2,1)} %bitcast.30), channel_id=1, source_target_pairs={{0,8},{8,0},{16,24},{24,16},{1,9},{9,1},{17,25},{25,17},{2,10},{10... | collective-permute-start | bytes 2359304 | tf_op jit(solution)/shard_map/ppermute | solution.py:34
  141.6 55.2 %collective-permute-start.1 = (bf16[2,256,768]{2,1,0:T(8,128)(2,1)}, bf16[2,256,768]{2,1,0:T(8,128)(2,1)S(1)}, u32[]{:S(2)}, u32[]{:S(2)}) collective-permute-start(bf16[2,256,768]{2,1,0:T(8,128)(2,1)} %bitcast.335), channel_id=1, source_target_pairs={{0,16},{8,24},{16,0},{24,8},{1,17},{9,25},{17,1},{25,9},{2,18},{10... | collective-permute-start | bytes 2359304 | tf_op jit(solution)/shard_map/ppermute | solution.py:34
  145.8 51.1 %collective-permute-start.2 = (bf16[2,256,768]{2,1,0:T(8,128)(2,1)}, bf16[2,256,768]{2,1,0:T(8,128)(2,1)S(1)}, u32[]{:S(2)}, u32[]{:S(2)}) collective-permute-start(bf16[2,256,768]{2,1,0:T(8,128)(2,1)} %bitcast.336), channel_id=1, source_target_pairs={{0,24},{8,16},{16,8},{24,0},{1,25},{9,17},{17,9},{25,1},{2,26},{10... | collective-permute-start | bytes 2359304 | tf_op jit(solution)/shard_map/ppermute | solution.py:34
  170.7 26.2 %copy-start.27 = (bf16[2,256,768]{2,1,0:T(8,128)(2,1)}, bf16[2,256,768]{2,1,0:T(8,128)(2,1)S(1)}, u32[]{:S(2)}) copy-start(bf16[2,256,768]{2,1,0:T(8,128)(2,1)S(1)} %collective-permute-done) | copy-start | bytes 2359300
  243.6 56.3 %all-to-all-start = ((bf16[2,1024,384]{2,0,1:T(2,128)(2,1)}), bf16[2,1024,384]{2,0,1:T(2,128)(2,1)}, u32[]{:S(2)}, u32[]{:S(2)}) async-start(bf16[2,1024,384]{2,0,1:T(2,128)(2,1)} %copy.86), calls=%async_computation | async-start | bytes 3145728 | tf_op jit(solution)/shard_map/all_to_all | solution.py:217
  394.4 10.9 copy-start.9
  405.4 12.0 copy-start.6
  430.3 42.1 %all-to-all-start.1 = ((bf16[2,256,1536]{1,0,2:T(2,128)(2,1)}), bf16[2,256,1536]{1,0,2:T(2,128)(2,1)}, u32[]{:S(2)}, u32[]{:S(2)}) async-start(bf16[2,256,1536]{1,0,2:T(2,128)(2,1)} %copy.88), calls=%async_computation.1 | async-start | bytes 3145728 | tf_op jit(solution)/shard_map/all_to_all | solution.py:285
  434.9 270.1 %reduce-scatter.14.cloned.1.call-start = ((), (), s32[]{:S(2)}) async-start(), calls=%async_computation.20 | async-start | bytes 5308416 | tf_op jit(solution)/shard_map/reduce_scatter | solution.py:325
  442.1 262.9 %reduce-scatter.10.cloned.1.call-start = ((), (), s32[]{:S(2)}) async-start(), calls=%async_computation.18 | async-start | bytes 2654208 | tf_op jit(solution)/shard_map/reduce_scatter | solution.py:319
  472.4 7.6 copy-start.39
  491.0 10.1 copy-start.4
  507.3 8.3 copy-start.3
  527.3 10.1 copy-start.4
  543.5 8.3 copy-start.3
  655.1 86.8 %reduce-scatter.12.cloned.1.call-start = ((), (), s32[]{:S(2)}) async-start(), calls=%async_computation.19 | async-start | bytes 2654208 | tf_op jit(solution)/shard_map/reduce_scatter | solution.py:322
  659.6 139.5 %reduce-scatter.8.cloned.1.call-start = ((), (), s32[]{:S(2)}) async-start(), calls=%async_computation.17 | async-start | bytes 5308416 | tf_op jit(solution)/shard_map/reduce_scatter | solution.py:316
  666.2 228.7 %reduce-scatter.16.cloned.1.call-start = ((), (), s32[]{:S(2)}) async-start(), calls=%async_computation.21 | async-start | bytes 14155776 | tf_op jit(solution)/shard_map/reduce_scatter | solution.py:267
  679.4 311.2 %reduce-scatter.18.cloned.1.call-start = ((), (), s32[]{:S(2)}) async-start(), calls=%async_computation.22 | async-start | bytes 14155776 | tf_op jit(solution)/shard_map/reduce_scatter | solution.py:270
  691.4 394.9 %reduce-scatter.20.cloned.1.call-start = ((), (), s32[]{:S(2)}) async-start(), calls=%async_computation.23 | async-start | bytes 14155776 | tf_op jit(solution)/shard_map/reduce_scatter | solution.py:273
  704.9 613.8 %all-reduce.10.cloned.1.call-start = ((), (), s32[]{:S(2)}) async-start(), calls=%async_computation.24 | async-start | bytes 12976128 | tf_op jit(solution)/shard_map/psum | solution.py:332
  1088.2 12.3 copy-start.19
  (36 other events, 106.8 us)
Sparse Core Ops, SparseCore 0:
  9.9 31.8 all-gather.9
  43.6 28.8 all-gather.11
  74.4 38.7 all-gather.7
  115.0 38.7 all-gather.13
  155.5 71.9 all-gather.15
  229.3 71.9 all-gather.17
  303.2 71.9 all-gather.19
  442.2 54.2 reduce-scatter.13
  655.2 40.4 reduce-scatter.9
  699.5 42.3 reduce-scatter.11
  745.3 53.7 reduce-scatter.7
  802.5 92.2 reduce-scatter.15
  898.3 92.2 reduce-scatter.17
  994.0 92.2 reduce-scatter.19
  1089.1 229.5 all-reduce.9
